TPU v7x, 256 devices: a whole 4x4x8 slice. The times are simulated.
256 devices in a mesh: layer: 4 (over z_lo, core), feat: 64 (over y, z_hi, x).
Axes of the slice: x: 4, y: 4, z: 8 (z_hi: 4, z_lo: 2; z = z_hi * 2 + z_lo), core: 2. Of those that a mesh axis runs over, the one named last changes fastest.
Arguments:
- activations: bfloat16 [512, 4, 2304], P('feat', 'layer'), may hold values from -6 to 6
- enc_weight: bfloat16 [4, 2304, 65536], P('layer', None, 'feat'), may hold values from -0.0625 to 0.0625
- dec_weight: bfloat16 [4, 65536, 2304], P('layer', 'feat'), may hold values from -0.03125 to 0.03125
- enc_bias: float32 [65536], P('feat'), may hold values from -3 to 3
- threshold: float32 [65536], P('feat'), may hold values from 0.1 to 1
- dec_bias: float32 [4, 2304], P('layer'), may hold values from -3 to 3
- token_mask: int32 [512], replicated, may hold values 0 or 1
Outputs:
- squared_error: float32 [512, 4], P('feat', 'layer')
- latent_grad: float32 [512, 65536], P(None, 'feat')
- input_grad: bfloat16 [512, 4, 2304], P('feat', 'layer')
All inputs are finite; a program needn't handle non-finite values.
Results may differ from a plain program's by a relative error of at most 0.015.
Values may be sent and summed in bfloat16 or wider, within the bound.
A program may use at most 64 MiB of HBM per device.

v0:
```python
import jax
import jax.numpy as jnp
from jax import lax
from jax.sharding import Mesh
from jax.sharding import PartitionSpec as P

FEAT = ("feat_0", "feat_1", "feat_2")


jump_scale = 0.25


def split_up(array, dim, length):
    before, after = (array.shape[:dim], array.shape[dim + 1 :])
    return jnp.moveaxis(array.reshape(*before, length, -1, *after), dim, 0)


def sent_and_summed(array, axis, dim):
    length = lax.axis_size(axis)
    parts = lax.all_to_all(split_up(array, dim, length), axis, 0, 0, tiled=True)
    return jnp.sum(parts, axis=0)


def sum_by_axis(array, axes, dim):
    far, near = axes
    parts = split_up(array, dim, lax.axis_size(far))
    nearer = sent_and_summed(parts, near, dim + 1)
    arrived = lax.all_to_all(nearer, far, split_axis=0, concat_axis=0, tiled=True)
    return arrived.sum(axis=0)


def shards(activations, enc_weight, dec_weight, enc_bias, threshold, dec_bias, token_mask):
    tok_dev = activations.shape[0]
    partial_value = jnp.einsum(
        "tld,ldf->tf",
        lax.all_gather(activations, FEAT, axis=0, tiled=True),
        enc_weight,
        preferred_element_type=jnp.float32,
    )
    preact = lax.psum(partial_value.astype(jnp.bfloat16), "layer").astype(jnp.float32) + enc_bias
    gating = jax.nn.sigmoid((preact - threshold) / jump_scale)
    latent = (preact * gating).astype(jnp.bfloat16)
    gate_slope = gating + preact * gating * (1.0 - gating) / jump_scale
    first_row = lax.axis_index(FEAT) * tok_dev
    rows = latent
    rebuilt = sum_by_axis(
        jnp.einsum("tf,lfd->tld", rows, dec_weight, preferred_element_type=jnp.float32),
        (("feat_0", "feat_1"), "feat_2"),
        0,
    )
    own_mask = lax.dynamic_slice_in_dim(token_mask, first_row, tok_dev, 0).astype(jnp.float32)[
        :, None, None
    ]
    error = own_mask * (rebuilt + dec_bias[None, :, :] - activations.astype(jnp.float32))
    grad_part = jnp.einsum(
        "tld,lfd->tf",
        lax.all_gather(error.astype(jnp.bfloat16), FEAT, axis=0, tiled=True),
        dec_weight,
        preferred_element_type=jnp.float32,
    )
    squared_error = jnp.mean(error * error, axis=-1)
    latent_grad = lax.psum(grad_part.astype(jnp.bfloat16), "layer").astype(jnp.float32)
    preact_grad = (latent_grad * gate_slope).astype(jnp.bfloat16)
    rows = preact_grad
    grad_terms = sum_by_axis(
        jnp.einsum("tf,ldf->tld", rows, enc_weight, preferred_element_type=jnp.float32),
        (("feat_0", "feat_1"), "feat_2"),
        0,
    )
    input_grad = (grad_terms - error).astype(jnp.bfloat16)
    return (squared_error, latent_grad, input_grad)


def solution(mesh):
    finer = Mesh(
        mesh.devices.reshape(mesh.shape["layer"], 4, 4, 4), ("layer", "feat_0", "feat_1", "feat_2")
    )
    return jax.shard_map(
        shards,
        mesh=finer,
        in_specs=(
            P(FEAT, "layer", None),
            P("layer", None, FEAT),
            P("layer", FEAT, None),
            P(FEAT),
            P(FEAT),
            P("layer", None),
            P(),
        ),
        out_specs=(P(FEAT, "layer"), P(None, FEAT), P(FEAT, "layer", None)),
        check_vma=False,
    )
```

profile of v0, /device:TPU:64, one launch (start us, length us, event | category | flops | bytes accessed | tf_op | source)
XLA Modules:
  0.0 494.5 jit_solution(7002110068138016690)
XLA Ops:
  7.2 0.7 all-gather.3.cloned.1.call-update
  8.0 85.3 %all-gather.3.cloned.1.call-done = bf16[512,1,2304]{2,0,1:T(8,128)(2,1)} async-done(((bf16[8,1,2304]{2,0,1:T(8,128)(2,1)}), bf16[512,1,2304]{2,0,1:T(8,128)(2,1)}) %all-gather.3.cloned.1.call-update) | async-done | bytes 2359312 | tf_op jit(solution)/shard_map/all_gather | solution.py:36
  93.3 6.6 %fusion.10 = bf16[512,1024]{1,0:T(8,128)(2,1)} fusion(bf16[1,2304,1024]{2,1,0:T(8,128)(2,1)} %param.8, bf16[512,1,2304]{2,0,1:T(8,128)(2,1)} %all-gather.3.cloned.1.call-done), kind=kOutput, calls=%fused_computation.15 | convolution fusion | flops 2416443392 | bytes 8126464 | tf_op jit(solution)/shard_map/tld,ldf->tf/dot_general | solution.py:34
  99.9 43.5 %all-reduce.3.cloned.1.call-done = bf16[512,1024]{1,0:T(8,128)(2,1)} async-done(((bf16[512,1024]{1,0:T(8,128)(2,1)}), bf16[512,1024]{1,0:T(8,128)(2,1)}) %all-reduce.3.cloned.1.call-update) | async-done | bytes 1048592 | tf_op jit(solution)/shard_map/psum | solution.py:40
  143.5 1.9 fusion.9
  145.3 4.9 convolution_bitcast_fusion.1
  150.3 0.4 copy.10
  150.7 59.1 %all_to_all.20 = f32[4,16,8,1,2304]{4,2,1,3,0:T(8,128)} all-to-all(f32[4,16,8,1,2304]{4,2,1,3,0:T(8,128)S(1)} %copy.10), channel_id=1, replica_groups=mesh['layer'=4,'feat_0'=4,'feat_1'=4,'feat_2'=4] {'feat_2'}, dimensions={0} | all-to-all | bytes 9437184 | tf_op jit(solution)/shard_map/all_to_all | solution.py:20
  209.8 3.7 reduce_sum.53
  213.5 9.4 %all-to-all-start.1 = ((f32[16,8,1,2304]{3,1,2,0:T(8,128)}), f32[16,8,1,2304]{3,1,2,0:T(8,128)S(1)}, u32[]{:S(2)}, u32[]{:S(2)}) async-start(f32[16,8,1,2304]{3,1,2,0:T(8,128)} %bitcast.8), calls=%async_computation.1 | async-start | bytes 2359296 | tf_op jit(solution)/shard_map/all_to_all | solution.py:28
  223.0 0.8 dynamic-slice_convert_fusion
  223.8 22.7 %all-to-all-done.1 = f32[16,8,1,2304]{3,1,2,0:T(8,128)S(1)} async-done(((f32[16,8,1,2304]{3,1,2,0:T(8,128)}), f32[16,8,1,2304]{3,1,2,0:T(8,128)S(1)}, u32[]{:S(2)}, u32[]{:S(2)}) %all-to-all-start.1) | async-done | bytes 1179680 | tf_op jit(solution)/shard_map/all_to_all | solution.py:28
  246.6 0.7 fusion.23
  247.5 81.1 %all-gather.5.cloned.1.call-done = bf16[512,1,2304]{2,0,1:T(8,128)(2,1)} async-done(((bf16[8,1,2304]{2,0,1:T(8,128)(2,1)}), bf16[512,1,2304]{2,0,1:T(8,128)(2,1)}) %all-gather.5.cloned.1.call-update) | async-done | bytes 2359312 | tf_op jit(solution)/shard_map/all_gather | solution.py:57
  328.6 6.7 %fusion.15 = bf16[512,1024]{1,0:T(8,128)(2,1)} fusion(bf16[1,1024,2304]{2,1,0:T(8,128)(2,1)} %param.9, bf16[512,1,2304]{2,0,1:T(8,128)(2,1)} %all-gather.5.cloned.1.call-done), kind=kOutput, calls=%fused_computation.16 | convolution fusion | flops 2416443392 | bytes 8126464 | tf_op jit(solution)/shard_map/tld,lfd->tf/dot_general | solution.py:55
  335.3 43.5 %all-reduce.5.cloned.1.call-done = bf16[512,1024]{1,0:T(8,128)(2,1)} async-done(((bf16[512,1024]{1,0:T(8,128)(2,1)}), bf16[512,1024]{1,0:T(8,128)(2,1)}) %all-reduce.5.cloned.1.call-update) | async-done | bytes 1048592 | tf_op jit(solution)/shard_map/psum | solution.py:62
  378.7 3.6 multiply_convert_fusion
  382.4 5.0 %convolution_bitcast_fusion = f32[4,16,8,1,2304]{4,2,0,1,3:T(8,128)S(1)} fusion(bf16[16,4,8,1024]{3,2,1,0:T(8,128)(2,1)S(1)} %bitcast.65, bf16[1,2304,1024]{2,1,0:T(8,128)(2,1)} %param.8), kind=kOutput, calls=%fused_computation | convolution fusion | flops 2415919104 | bytes 10485760 | tf_op jit(solution)/shard_map/tf,ldf->tld/dot_general | solution.py:66
  387.4 0.4 copy.11
  387.8 59.1 %all_to_all.21 = f32[4,16,8,1,2304]{4,2,1,3,0:T(8,128)} all-to-all(f32[4,16,8,1,2304]{4,2,1,3,0:T(8,128)S(1)} %copy.11), channel_id=1, replica_groups=mesh['layer'=4,'feat_0'=4,'feat_1'=4,'feat_2'=4] {'feat_2'}, dimensions={0} | all-to-all | bytes 9437184 | tf_op jit(solution)/shard_map/all_to_all | solution.py:20
  446.9 2.7 reduce_sum.58
  449.6 37.0 %all_to_all.22 = f32[16,8,1,2304]{3,1,2,0:T(8,128)S(1)} all-to-all(f32[16,8,1,2304]{3,1,2,0:T(8,128)S(1)} %bitcast.64), channel_id=1, replica_groups=mesh['layer'=4,'feat_0'=4,'feat_1'=4,'feat_2'=4] {'feat_0','feat_1'}, dimensions={0} | all-to-all | bytes 2359296 | tf_op jit(solution)/shard_map/all_to_all | solution.py:28
  486.7 0.8 fusion.20
  487.5 0.5 multiply_bitcast_fusion
  (20 shorter events, 0.6 us)
Async XLA Ops:
  7.2 86.1 %all-gather.3.cloned.1.call-start = ((), (), s32[]{:S(2)}) async-start(), calls=%async_computation.4 | async-start | bytes 2396160 | tf_op jit(solution)/shard_map/all_gather | solution.py:36
  7.9 135.6 %copy-start.2 = (f32[1024]{0:T(1024)S(1)}, f32[1024]{0:T(1024)}, u32[]{:S(2)}) copy-start(f32[1024]{0:T(1024)} %param.11) | copy-start | bytes 12292
  7.9 135.5 %copy-start.3 = (f32[1024]{0:T(1024)S(1)}, f32[1024]{0:T(1024)}, u32[]{:S(2)}) copy-start(f32[1024]{0:T(1024)} %param.10) | copy-start | bytes 12292
  7.9 135.5 %all-reduce.3.cloned.1.call-start = ((), (), s32[]{:S(2)}) async-start(), calls=%async_computation.5 | async-start | bytes 2097152 | tf_op jit(solution)/shard_map/psum | solution.py:40
  213.5 9.5 %copy-start.4 = (f32[1,2304]{1,0:T(1,128)S(1)}, f32[1,2304]{1,0:T(1,128)}, u32[]{:S(2)}) copy-start(f32[1,2304]{1,0:T(1,128)} %param.12) | copy-start | bytes 27652
  213.5 33.0 %copy-start.1 = (bf16[8,1,2304]{2,0,1:T(8,128)(2,1)S(1)}, bf16[8,1,2304]{2,0,1:T(8,128)(2,1)}, u32[]{:S(2)}) copy-start(bf16[8,1,2304]{2,0,1:T(8,128)(2,1)} %param.7) | copy-start | bytes 110596
  213.5 33.0 %all-to-all-start.1 = ((f32[16,8,1,2304]{3,1,2,0:T(8,128)}), f32[16,8,1,2304]{3,1,2,0:T(8,128)S(1)}, u32[]{:S(2)}, u32[]{:S(2)}) async-start(f32[16,8,1,2304]{3,1,2,0:T(8,128)} %bitcast.8), calls=%async_computation.1 | async-start | bytes 2359296 | tf_op jit(solution)/shard_map/all_to_all | solution.py:28
  222.9 105.7 %all-gather.5.cloned.1.call-start = ((), (), s32[]{:S(2)}) async-start(), calls=%async_computation.6 | async-start | bytes 2396160 | tf_op jit(solution)/shard_map/all_gather | solution.py:57
  247.3 131.4 %copy-start = (bf16[512,1024]{1,0:T(8,128)(2,1)S(1)}, bf16[512,1024]{1,0:T(8,128)(2,1)}, u32[]{:S(2)}) copy-start(bf16[512,1024]{1,0:T(8,128)(2,1)} %all-reduce.3.cloned.1.call-done) | copy-start | bytes 3145732
  247.3 131.4 %all-reduce.5.cloned.1.call-start = ((), (), s32[]{:S(2)}) async-start(), calls=%async_computation.7 | async-start | bytes 2097152 | tf_op jit(solution)/shard_map/psum | solution.py:62
Sparse Core Ops, SparseCore 0:
  11.2 82.0 all-gather.2
  100.1 43.3 all-reduce.2
  247.4 81.1 all-gather.4
  335.4 43.2 all-reduce.4
where the time goes:
time: 499 us; the launch traced here: 495 us
  waiting for transfers between devices  277 us (56%)
  blocking collectives  155 us (31%)
  matrix products  23.2 us (5%)
  other arithmetic  14.9 us (3%)
  between operations  13.9 us (3%)
  starting transfers between devices  9.73 us (2%)
    all_to_all x2, blocking collectives, sent_and_summed(): parts = lax.all_to_all(split_up(array, dim, length), axis, 0, 0, tiled=True)  118 us
    all_gather x1, waiting for transfers between devices, shards(): lax.all_gather(activations, FEAT, axis=0, tiled=True)  85.3 us
    all_gather x1, waiting for transfers between devices, shards(): lax.all_gather(error.astype(jnp.bfloat16), FEAT, axis=0, tiled=True)  81.1 us
    psum x1, waiting for transfers between devices, shards(): lax.psum(partial_value.astype(jnp.bfloat16), 'layer').astype(jnp.float32)  43.5 us
    psum x1, waiting for transfers between devices, shards(): lax.psum(grad_part.astype(jnp.bfloat16), 'layer').astype(jnp.float32)  43.5 us
    all_to_all x1, blocking collectives, sum_by_axis(): lax.all_to_all(nearer, far, split_axis=0, concat_axis=0, tiled=True)  37 us
    all_to_all x1, waiting for transfers between devices, sum_by_axis(): lax.all_to_all(nearer, far, split_axis=0, concat_axis=0, tiled=True)  22.7 us
  transfers between devices with their start and end apart: 5, of which 5 were waited for; matrix products, arithmetic and copies ran while one was open for 0% of the time, Pallas kernels for 0%

commit v1 on v0

v1 whole, which is shorter than its diff:
```python
import functools

import jax
import jax.numpy as jnp
from jax import lax
from jax.experimental import pallas as pl
from jax.experimental.pallas import tpu as pltpu
from jax.sharding import Mesh
from jax.sharding import PartitionSpec as P

FEAT = ("y", "zh", "x")
LAYER = ("zl", "co")
MESH = pl.DeviceIdType.MESH
BF = jnp.bfloat16
F32 = jnp.float32
JUMP = 0.25

N = 4
C = 2
S = N // C
ROWS = 8
R = S * ROWS
M = N * N * R
HM = M // 2
LAG = 3


def kernel(
    acts, enc_hbm, dec_hbm, enc_bias, threshold, dec_bias, mask,
    sq_out, ig_out, lg_out,
    enc, dec, ag, zbuf, ps, f1, a1, b1, ps2, f2, a2, b2, ps3, zr,
    keep, dsend, drecv, zs, zv, full, lat, slope, err, errh,
    wsem, osem, zsnd, zrcv, agsnd, agrcv, rssnd, rsrcv, zrsnd, zrrcv, lsnd, lrcv,
):
    depth = ag.shape[-1]
    feats = lat.shape[-1]
    half = depth // 2
    cut = (half // 256 + 1) * 128
    x, y, zh = lax.axis_index("x"), lax.axis_index("y"), lax.axis_index("zh")
    zl, co = lax.axis_index("zl"), lax.axis_index("co")
    at = {"x": x, "y": y, "zh": zh}

    def step(axis, by):
        return lax.rem(at[axis] + (by + N) % N, N)

    def to(axis, by):
        return {axis: step(axis, by)}

    enc_copy = pltpu.make_async_copy(enc_hbm, enc, wsem.at[0])
    dec_copy = pltpu.make_async_copy(dec_hbm, dec, wsem.at[1])
    enc_copy.start()
    dec_copy.start()

    barrier = pltpu.get_barrier_semaphore()
    peers = [to("x", 1), to("x", -1), to("y", 1), to("y", -1)]
    peers += [to("zh", 1), to("zh", 2), to("zh", 3), {"zl": 1 - zl}, {"co": 1 - co}]
    for peer in peers:
        pl.semaphore_signal(barrier, inc=1, device_id=peer, device_id_type=MESH)
    pl.semaphore_wait(barrier, len(peers))

    def remote(src, dst, send, recv, peer):
        return pltpu.make_async_remote_copy(
            src_ref=src, dst_ref=dst, send_sem=send, recv_sem=recv,
            device_id=peer, device_id_type=MESH,
        )

    def cols(h, part):
        base, length = {None: (0, half), 0: (0, cut), 1: (cut, half - cut)}[part]
        return pl.ds(h * half + base, length)

    class Gather:
        def __init__(self, axis, block, send, recv):
            self.axis, self.block, self.send, self.recv = axis, block, send, recv
            self.copies = []

        def push(self, pos, part, by):
            n = len(self.copies)
            ref = self.block(pos, part)
            copy = remote(ref, ref, self.send.at[n], self.recv.at[n], to(self.axis, by))
            copy.start()
            self.copies.append(copy)

        def start(self):
            self.push(at[self.axis], None, 1)
            self.push(at[self.axis], None, -1)

        def middle(self):
            self.copies[0].wait_recv()
            self.push(step(self.axis, -1), 0, 1)
            self.copies[1].wait_recv()
            self.push(step(self.axis, 1), 1, -1)

        def finish(self):
            self.copies[2].wait_recv()
            self.copies[3].wait_recv()
            for copy in self.copies:
                copy.wait_send()

    class Scatter:
        def __init__(self, axis, block, f, a, b, send, recv):
            self.axis, self.block, self.f, self.a, self.b = axis, block, f, a, b
            self.send, self.recv, self.copies = send, recv, []

        def push(self, src, dst, by):
            n = len(self.copies)
            copy = remote(src, dst, self.send.at[n], self.recv.at[n], to(self.axis, by))
            copy.start()
            self.copies.append(copy)

        def slot(self, buf, part):
            return buf.at[(slice(None),) * (len(buf.shape) - 1) + (cols(0, part),)]

        def start(self):
            far = step(self.axis, 2)
            self.push(self.block(far, 0), self.slot(self.f, 0), 1)
            self.push(self.block(far, 1), self.slot(self.f, 1), -1)
            self.push(self.block(step(self.axis, 1), 1), self.slot(self.a, 1), 1)
            self.push(self.block(step(self.axis, -1), 0), self.slot(self.b, 0), -1)

        def middle(self):
            for part, by, into in ((0, 1, self.a), (1, -1, self.b)):
                self.copies[part].wait_recv()
                here = self.slot(self.f, part)
                own = self.block(step(self.axis, by), part)
                here[...] = (here[...].astype(F32) + own[...].astype(F32)).astype(BF)
                self.push(here, self.slot(into, part), by)

        def finish(self):
            for copy in self.copies[2:]:
                copy.wait_recv()
            total = self.block(at[self.axis], None)[...].astype(F32)
            total = total + self.a[...].astype(F32) + self.b[...].astype(F32)
            for copy in self.copies:
                copy.wait_send()
            return total

    def chunk(c):
        def z_send(src):
            for s in range(S):
                @pl.when(zh == c * S + s)
                def _():
                    zbuf[c, s] = src[...]
                    for k in (1, 2, 3):
                        remote(src, zbuf.at[c, s], zsnd.at[k - 1], zrcv.at[c, s], to("zh", k)).start()

        def z_wait(src):
            for s in range(S):
                one = remote(src, zbuf.at[c, s], zsnd.at[0], zrcv.at[c, s], to("zh", 1))

                @pl.when(zh != c * S + s)
                def _():
                    one.wait_recv()

                @pl.when(zh == c * S + s)
                def _():
                    for k in (1, 2, 3):
                        remote(src, zbuf.at[c, s], zsnd.at[k - 1], zrcv.at[c, s], to("zh", k)).wait_send()

            ag[c, y, x] = zbuf[c].astype(F32).reshape(R, depth).astype(BF)

        def gather_stages(src):
            near = [
                Gather("x", lambda i, p: ag.at[c, y, i, :, cols(0, p)], agsnd.at[c, 0, 0], agrcv.at[c, 0, 0]),
                Gather("y", lambda i, p: ag.at[c, i, x, :, cols(1, p)], agsnd.at[c, 1, 0], agrcv.at[c, 1, 0]),
            ]
            wide = [
                Gather("y", lambda i, p: ag.at[c, i, :, :, cols(0, p)], agsnd.at[c, 0, 1], agrcv.at[c, 0, 1]),
                Gather("x", lambda i, p: ag.at[c, :, i, :, cols(1, p)], agsnd.at[c, 1, 1], agrcv.at[c, 1, 1]),
            ]

            def begin():
                z_wait(src)
                for g in near:
                    g.start()

            def forward():
                for g in near:
                    g.middle()

            def widen():
                for g, w in zip(near, wide):
                    g.finish()
                    w.start()

            def forward_wide():
                for w in wide:
                    w.middle()

            def end():
                for w in wide:
                    w.finish()

            return [begin, forward, widen, forward_wide, end]

        def layer_stages(lhs, rhs, tile):
            copies = {}

            def multiply():
                def one(j, carry):
                    where = pl.ds(pl.multiple_of(j * tile, tile), tile)
                    value = rhs(lhs, where)
                    low, high = value[:HM], value[HM:]
                    keep[c, :, where] = jnp.where(co == 0, low, high)
                    dsend[c, :, where] = jnp.where(co == 0, high, low).astype(BF)
                    return carry

                lax.fori_loop(0, feats // tile, one, 0)
                copies[0] = remote(dsend.at[c], drecv.at[c], lsnd.at[c, 0], lrcv.at[c, 0], {"co": 1 - co})
                copies[0].start()

            def pair():
                copies[0].wait()
                zs[c] = (keep[c] + drecv[c].astype(F32)).astype(BF)
                copies[1] = remote(zs.at[c], zv.at[c], lsnd.at[c, 1], lrcv.at[c, 1], {"zl": 1 - zl})
                copies[1].start()

            def share():
                copies[1].wait()
                full[c, co] = (zs[c].astype(F32) + zv[c].astype(F32)).astype(BF)
                ref = full.at[c, co]
                copies[2] = remote(ref, ref, lsnd.at[c, 2], lrcv.at[c, 2], {"co": 1 - co})
                copies[2].start()

            def end():
                copies[2].wait()

            return [multiply, pair, share, end]

        def scatter_stages(multiply):
            wide = [
                Scatter("y", lambda i, p: ps.at[c, i, :, :, cols(0, p)], f1.at[c, 0], a1.at[c, 0], b1.at[c, 0],
                        rssnd.at[c, 0, 0], rsrcv.at[c, 0, 0]),
                Scatter("x", lambda i, p: ps.at[c, :, i, :, cols(1, p)], f1.at[c, 1], a1.at[c, 1], b1.at[c, 1],
                        rssnd.at[c, 1, 0], rsrcv.at[c, 1, 0]),
            ]
            near = [
                Scatter(axis, lambda i, p, h=h: ps2.at[c, h, i, :, cols(0, p)], f2.at[c, h], a2.at[c, h], b2.at[c, h],
                        rssnd.at[c, h, 1], rsrcv.at[c, h, 1])
                for h, axis in enumerate(("x", "y"))
            ]

            def begin():
                for h in range(2):
                    multiply(h)
                    wide[h].start()

            def forward():
                for w in wide:
                    w.middle()

            def narrow():
                for h in range(2):
                    ps2[c, h] = wide[h].finish().astype(BF)
                    near[h].start()

            def forward_near():
                for g in near:
                    g.middle()

            def z_out():
                for h in range(2):
                    ps3[c, :, :, cols(h, None)] = near[h].finish().reshape(S, ROWS, half).astype(BF)
                for s in range(S):
                    @pl.when(zh != c * S + s)
                    def _():
                        k = lax.rem(zh - (c * S + s) + N, N) - 1
                        remote(ps3.at[c, s], zr.at[k], zrsnd.at[c, s], zrrcv.at[k], {"zh": c * S + s}).start()

            return [begin, forward, narrow, forward_near, z_out]

        def owned(then):
            for s in range(S):
                @pl.when(zh != c * S + s)
                def _():
                    remote(ps3.at[c, s], zr.at[0], zrsnd.at[c, s], zrrcv.at[0], {"zh": c * S + s}).wait_send()

                @pl.when(zh == c * S + s)
                def _():
                    total = ps3[c, s].astype(F32)
                    for k in range(3):
                        remote(ps3.at[c, s], zr.at[k], zrsnd.at[c, s], zrrcv.at[k], to("zh", 1)).wait_recv()
                        total = total + zr[k].astype(F32)
                    then(total)

        def z_first():
            z_send(acts)

        def to_latent():
            for r in range(2):
                preact = full[c, r].astype(F32) + enc_bias[...]
                gating = jax.nn.sigmoid((preact - threshold[...]) * (1.0 / JUMP))
                value = preact * gating
                lat[c, pl.ds(r * HM, HM)] = value.astype(BF)
                slope[c, pl.ds(r * HM, HM)] = gating + value * (1.0 - gating) * (1.0 / JUMP)

        def to_preact_grad():
            pltpu.make_async_copy(full.at[c], lg_out.at[c], osem.at[c]).start()
            for r in range(2):
                rows = pl.ds(r * HM, HM)
                lat[c, rows] = (full[c, r].astype(F32) * slope[c, rows]).astype(BF)

        def to_error():
            def then(total):
                row = lax.broadcasted_iota(jnp.int32, (ROWS, 1), 0)
                first = ((y * N + zh) * N + x) * ROWS
                keeps = jnp.zeros((ROWS, 1), jnp.int32)
                for i in range(ROWS):
                    keeps = jnp.where(row == i, mask[first + i], keeps)
                value = keeps.astype(F32) * (total + dec_bias[...] - acts[...].astype(F32))
                err[...] = value
                errh[...] = value.astype(BF)
                sq_out[...] = jnp.sum(value * value, axis=1, keepdims=True) * (1.0 / depth)

            owned(then)
            z_send(errh)

        def to_input_grad():
            def then(total):
                ig_out[...] = (total - err[...]).astype(BF)

            owned(then)

        def dot(a, b, dims):
            return lax.dot_general(a, b, (dims, ((), ())), preferred_element_type=F32)

        def tokens():
            return ag[c].reshape(M, depth)

        def encode(lhs, where):
            return dot(lhs(), enc[:, where], ((1,), (0,)))

        def decode_back(lhs, where):
            return dot(lhs(), dec[where, :], ((1,), (1,)))

        def tiles(h):
            begin = 0
            while begin < half:
                length = min(512, half - begin)
                yield pl.ds(h * half + begin, length), length
                begin += length

        def decode(h):
            for where, length in tiles(h):
                value = dot(lat[c], dec[:, where], ((1,), (0,)))
                ps[c, :, :, :, where] = value.reshape(N, N, R, length).astype(BF)

        def encode_back(h):
            for where, length in tiles(h):
                value = dot(lat[c], enc[where, :], ((1,), (1,)))
                ps[c, :, :, :, where] = value.reshape(N, N, R, length).astype(BF)

        def wait_enc():
            if c == 0:
                enc_copy.wait()

        def wait_dec():
            if c == 0:
                dec_copy.wait()

        def joined(*parts):
            def run():
                for part in parts:
                    part()

            return run

        g1, l1, s1 = gather_stages(acts), layer_stages(tokens, encode, 256), scatter_stages(decode)
        g2, l2, s2 = gather_stages(errh), layer_stages(tokens, decode_back, 256), scatter_stages(encode_back)
        return [
            z_first,
            *g1[:-1],
            joined(g1[-1], wait_enc, l1[0]),
            *l1[1:-1],
            joined(l1[-1], to_latent, wait_dec, s1[0]),
            *s1[1:],
            to_error,
            *g2[:-1],
            joined(g2[-1], l2[0]),
            *l2[1:-1],
            joined(l2[-1], to_preact_grad, s2[0]),
            *s2[1:],
            to_input_grad,
        ]

    plans = [chunk(c) for c in range(C)]
    length = len(plans[0])
    for tick in range(length + LAG * (C - 1)):
        for c in range(C):
            if 0 <= tick - LAG * c < length:
                plans[c][tick - LAG * c]()
    for c in range(C):
        pltpu.make_async_copy(full.at[c], lg_out.at[c], osem.at[c]).wait()


def shards(activations, enc_weight, dec_weight, enc_bias, threshold, dec_bias, token_mask):
    depth, feats = enc_weight.shape[1:]
    half = depth // 2
    vmem, any_space = pl.BlockSpec(memory_space=pltpu.VMEM), pl.BlockSpec(memory_space=pl.ANY)
    dma = pltpu.SemaphoreType.DMA
    scratch = [
        pltpu.VMEM((depth, feats), BF),
        pltpu.VMEM((feats, depth), BF),
        pltpu.VMEM((C, N, N, R, depth), BF),
        pltpu.VMEM((C, S, ROWS, depth), BF),
        pltpu.VMEM((C, N, N, R, depth), BF),
        *[pltpu.VMEM((C, 2, N, R, half), BF)] * 3,
        pltpu.VMEM((C, 2, N, R, half), BF),
        *[pltpu.VMEM((C, 2, R, half), BF)] * 3,
        pltpu.VMEM((C, S, ROWS, depth), BF),
        pltpu.VMEM((N - 1, ROWS, depth), BF),
        pltpu.VMEM((C, HM, feats), F32),
        *[pltpu.VMEM((C, HM, feats), BF)] * 4,
        pltpu.VMEM((C, 2, HM, feats), BF),
        pltpu.VMEM((C, M, feats), BF),
        pltpu.VMEM((C, M, feats), F32),
        pltpu.VMEM((ROWS, depth), F32),
        pltpu.VMEM((ROWS, depth), BF),
        dma((2,)),
        dma((C,)),
        dma((3,)), dma((C, S)),
        dma((C, 2, 2, 4)), dma((C, 2, 2, 4)),
        dma((C, 2, 2, 6)), dma((C, 2, 2, 6)),
        dma((C, S)), dma((3,)),
        dma((C, 3)), dma((C, 3)),
    ]
    sq, ig, lg = pl.pallas_call(
        kernel,
        out_shape=(
            jax.ShapeDtypeStruct((ROWS, 1), F32),
            jax.ShapeDtypeStruct((ROWS, depth), BF),
            jax.ShapeDtypeStruct((C, 2, HM, feats), BF),
        ),
        in_specs=[vmem, any_space, any_space, vmem, vmem, vmem, pl.BlockSpec(memory_space=pltpu.SMEM)],
        out_specs=(vmem, vmem, any_space),
        scratch_shapes=scratch,
        compiler_params=pltpu.CompilerParams(
            collective_id=0, has_side_effects=True, vmem_limit_bytes=48 * 1024 * 1024
        ),
    )(
        activations[:, 0], enc_weight[0], dec_weight[0], enc_bias[None], threshold[None], dec_bias, token_mask,
    )
    lg = lg.reshape(C, N, N, S, ROWS, feats).transpose(1, 0, 3, 2, 4, 5)
    return sq, lg.reshape(N * N * N * ROWS, feats).astype(F32), ig[:, None]


def solution(mesh):
    finer = Mesh(mesh.devices.reshape(2, 2, N, N, N), LAYER + FEAT)
    return jax.shard_map(
        shards,
        mesh=finer,
        in_specs=(
            P(FEAT, LAYER, None),
            P(LAYER, None, FEAT),
            P(LAYER, FEAT, None),
            P(FEAT),
            P(FEAT),
            P(LAYER, None),
            P(),
        ),
        out_specs=(P(FEAT, LAYER), P(None, FEAT), P(FEAT, LAYER, None)),
        check_vma=False,
    )
```

time: 499 us -> 147 us (0.29)
  waiting for transfers between devices: 277 us -> 0 us
  blocking collectives: 155 us -> 0 us
  Pallas kernels: 0 us -> 136 us
  matrix products: 23.2 us -> 0 us
  other arithmetic: 14.9 us -> 0.24 us
  between operations: 13.9 us -> 0.66 us
  starting transfers between devices: 9.73 us -> 0 us
  local copies, waits for them, and re-layouts: 0.84 us -> 8.51 us
    all_gather x2 -> x0, waiting for transfers between devices: 166 us -> none  [the longest x1 85.3 us: shards(): lax.all_gather(activations, FEAT, axis=0, tiled=True)]
    all_to_all x3 -> x0, blocking collectives: 155 us -> none  [the longest x2 118 us: sent_and_summed(): parts = lax.all_to_all(split_up(array, dim, length), axis, 0, 0, tiled=True)]
    pallas_call x0 -> x1, Pallas kernels: none -> 136 us  [shards(): pl.pallas_call(kernel, out_shape=(jax.ShapeDtypeStruct((ROWS, 1), F32), j...]
    psum x2 -> x0, waiting for transfers between devices: 87 us -> none  [the longest x1 43.5 us: shards(): lax.psum(partial_value.astype(jnp.bfloat16), 'layer').astype(jnp.float32)]
    dot_general x4 -> x0, matrix products: 23.2 us -> none  [the longest x1 6.65 us: shards(): jnp.einsum('tld,lfd->tf', lax.all_gather(error.astype(jnp.bfloat16), FEAT...]
    all_to_all x1 -> x0, waiting for transfers between devices: 22.7 us -> none  [sum_by_axis(): lax.all_to_all(nearer, far, split_axis=0, concat_axis=0, tiled=True)]
    all_to_all x1 -> x0, starting transfers between devices: 9.4 us -> none  [sum_by_axis(): lax.all_to_all(nearer, far, split_axis=0, concat_axis=0, tiled=True)]
    convert_element_type x5 -> x1, other arithmetic: 7.76 us -> 0.24 us  [shards(): return (sq, lg.reshape(N * N * N * ROWS, feats).astype(F32), ig[:, None])]
  transfers between devices with their start and end apart: 5 -> 0, of which waited for: 5 -> 0; matrix products, arithmetic and copies ran while one was open for 0% -> 0% of each run, Pallas kernels for 0% -> 0%
where the time goes in v1:
time: 147 us; the launch traced here: 146 us
  Pallas kernels  136 us (93%)
  local copies, waits for them, and re-layouts  8.51 us (6%)
    pallas_call x1, Pallas kernels, shards(): pl.pallas_call(kernel, out_shape=(jax.ShapeDtypeStruct((ROWS, 1), F32), j...  136 us
    unnamed x14, local copies, waits for them, and re-layouts  7.05 us

profile of v1, /device:TPU:64, one launch (start us, length us, event | category | flops | bytes accessed | tf_op | source)
XLA Modules:
  0.0 145.8 jit_solution(14506799361721670576)
XLA Ops:
  0.6 0.0 copy-start
  0.6 2.3 %copy-done = bf16[1,2304,1024]{2,1,0:T(8,128)(2,1)S(1)} copy-done((bf16[1,2304,1024]{2,1,0:T(8,128)(2,1)S(1)}, bf16[1,2304,1024]{2,1,0:T(8,128)(2,1)}, u32[]{:S(2)}) %copy-start) | copy-done | bytes 4718616
  3.0 0.0 copy-start.1
  3.0 0.8 copy-done.1
  3.7 0.0 copy-start.2
  3.7 0.7 copy-done.2
  4.4 0.0 copy-start.3
  4.4 0.7 copy-done.3
  5.1 0.0 copy-start.4
  5.1 0.7 copy-done.4
  5.8 0.0 copy-start.5
  5.8 0.7 copy-done.5
  6.5 136.4 %shard_map.94 = (f32[8,1]{1,0:T(8,128)S(1)}, bf16[8,2304]{1,0:T(8,128)(2,1)S(1)}, bf16[2,2,128,1024]{3,2,1,0:T(8,128)(2,1)S(1)}) custom-call(bf16[8,2304]{1,0:T(8,128)(2,1)S(1)} %bitcast.13, bf16[2304,1024]{1,0:T(8,128)(2,1)S(1)} %bitcast.11, bf16[1024,2304]{1,0:T(8,128)(2,1)} %bitcast.17, f32[1,1024]{1,0:T(1,128)S(1)} %bitcast.15, f32[1,1024]{1,0:T(1,128)S(1)} %bitcast.16, ...), custom_call_target="tpu_custom_call" | custom-call | tf_op jit(solution)/shard_map/pallas_call | solution.py:426
  142.9 0.6 copy.11
  143.5 0.2 convert_bitcast_fusion
  143.7 1.5 %copy.10 = f32[4,2,2,4,8,1024]{5,4,3,2,1,0:T(8,128)} copy(f32[4,2,2,4,8,1024]{5,4,2,3,0,1:T(8,128)S(1)} %convert_bitcast_fusion) | data formatting | bytes 4194304 | tf_op jit(solution)/shard_map/convert_element_type | solution.py:443
  145.2 0.6 copy.13
Async XLA Ops:
  0.6 2.3 %copy-start = (bf16[1,2304,1024]{2,1,0:T(8,128)(2,1)S(1)}, bf16[1,2304,1024]{2,1,0:T(8,128)(2,1)}, u32[]{:S(2)}) copy-start(bf16[1,2304,1024]{2,1,0:T(8,128)(2,1)} %param.8) | copy-start | bytes 14155780
  3.0 0.8 copy-start.1
  3.7 0.7 copy-start.2
  4.4 0.7 copy-start.3
  5.1 0.7 copy-start.4
  5.8 0.7 copy-start.5

commit v2 on v1

v2 whole, which is shorter than its diff:
```python
import functools

import jax
import jax.numpy as jnp
from jax import lax
from jax.experimental import pallas as pl
from jax.experimental.pallas import tpu as pltpu
from jax.sharding import Mesh
from jax.sharding import PartitionSpec as P

FEAT = ("y", "zh", "x")
LAYER = ("zl", "co")
MESH = pl.DeviceIdType.MESH
BF = jnp.bfloat16
F32 = jnp.float32
JUMP = 0.25

N = 4
C = 4
S = N // C
ROWS = 8
R = S * ROWS
M = N * N * R
HM = M // 2
PIECES = 2
TURNS = (
    0, 2, 1, 3, 0, 2, 1, 3, 0, 1, 0, 2, 1, 3, 0, 2, 0, 0, 1, 0, 3, 1, 1, 1, 2, 0, 2, 0, 2,
    3, 2, 0, 3, 1, 1, 3, 1, 0, 2, 3, 2, 2, 3, 1, 0, 2, 1, 3, 0, 2, 3, 1, 2, 0, 3, 1, 3, 2,
    0, 1, 3, 0, 2, 1, 0, 3, 1, 2, 0, 3, 0, 0, 2, 1, 0, 1, 3, 1, 2, 0, 1, 2, 3, 2, 0, 2, 1,
    0, 1, 3, 3, 3, 2, 2, 0, 3, 1, 2, 3, 3, 0, 3, 2, 0, 1, 3, 2, 1, 3, 2, 1, 3, 2, 1, 0, 3,
)


def kernel(
    acts_hbm, enc_hbm, dec_hbm, enc_bias_hbm, threshold_hbm, dec_bias_hbm, mask_hbm,
    sq_out, ig_out, lg_out,
    acts, enc_bias, threshold, dec_bias, mask, enc, dec, ag, zbuf, ps, f1, a1, b1, ps2, f2, a2, b2, ps3, zr,
    keep, dsend, drecv, zs, zv, full, lat, slope, err, errh, sq, ig,
    wsem, osem, zsnd, zrcv, agsnd, agrcv, rssnd, rsrcv, zrsnd, zrrcv, lsnd, lrcv,
):
    depth = ag.shape[-1]
    feats = lat.shape[-1]
    half = depth // 2
    cut = (half // 256 + 1) * 128
    x, y, zh = lax.axis_index("x"), lax.axis_index("y"), lax.axis_index("zh")
    zl, co = lax.axis_index("zl"), lax.axis_index("co")
    at = {"x": x, "y": y, "zh": zh}

    def step(axis, by):
        return lax.rem(at[axis] + (by + N) % N, N)

    def to(axis, by):
        return {axis: step(axis, by)}

    acts_copy, enc_copy, dec_copy, *small = [
        pltpu.make_async_copy(src, dst, wsem.at[n])
        for n, (src, dst) in enumerate((
            (acts_hbm, acts), (enc_hbm, enc), (dec_hbm, dec), (enc_bias_hbm, enc_bias),
            (threshold_hbm, threshold), (dec_bias_hbm, dec_bias), (mask_hbm, mask),
        ))
    ]
    for copy in (acts_copy, *small, enc_copy, dec_copy):
        copy.start()

    barrier = pltpu.get_barrier_semaphore()
    peers = [to(axis, by) for axis in ("x", "y", "zh") for by in (1, 2, 3)]
    peers += [{"zl": 1 - zl}, {"co": 1 - co}]
    for peer in peers:
        pl.semaphore_signal(barrier, inc=1, device_id=peer, device_id_type=MESH)
    pl.semaphore_wait(barrier, len(peers))
    acts_copy.wait()

    def remote(src, dst, send, recv, peer):
        return pltpu.make_async_remote_copy(
            src_ref=src, dst_ref=dst, send_sem=send, recv_sem=recv,
            device_id=peer, device_id_type=MESH,
        )

    def cols(h, part):
        base, length = {None: (0, half), 0: (0, cut), 1: (cut, half - cut)}[part]
        return pl.ds(h * half + base, length)

    class Ring:
        def __init__(self, axis, block, send, recv):
            self.axis, self.block, self.send, self.recv = axis, block, send, recv
            self.copies = []

        def push(self, src, dst, by):
            n = len(self.copies)
            copy = remote(src, dst, self.send.at[n], self.recv.at[n], to(self.axis, by))
            copy.start()
            self.copies.append(copy)

        def arrived(self, *which):
            for n in which:
                self.copies[n].wait_recv()

        def sent(self):
            for copy in self.copies:
                copy.wait_send()

    class Gather(Ring):
        def pass_on(self, pos, part, by):
            ref = self.block(pos, part)
            self.push(ref, ref, by)

        def start(self):
            me = at[self.axis]
            self.pass_on(me, 0, 1)
            self.pass_on(me, 1, -1)
            self.pass_on(me, 1, 1)
            self.pass_on(me, 0, -1)

        def middle(self):
            self.arrived(0)
            self.pass_on(step(self.axis, -1), 0, 1)
            self.arrived(1)
            self.pass_on(step(self.axis, 1), 1, -1)

        def finish(self):
            self.arrived(2, 3, 4, 5)
            self.sent()

    class DirectGather(Ring):
        def start(self):
            ref = self.block(at[self.axis], None)
            for by in (2, 1, -1):
                self.push(ref, ref, by)

        def finish(self):
            self.arrived(0, 1, 2)
            self.sent()

    class Scatter(Ring):
        def __init__(self, axis, block, f, a, b, send, recv):
            super().__init__(axis, block, send, recv)
            self.f, self.a, self.b = f, a, b

        def slot(self, buf, part):
            return buf.at[(slice(None),) * (len(buf.shape) - 1) + (cols(0, part),)]

        def start(self):
            far = step(self.axis, 2)
            self.push(self.block(far, 0), self.slot(self.f, 0), 1)
            self.push(self.block(far, 1), self.slot(self.f, 1), -1)
            self.push(self.block(step(self.axis, 1), 1), self.slot(self.a, 1), 1)
            self.push(self.block(step(self.axis, -1), 0), self.slot(self.b, 0), -1)

        def middle(self):
            for part, by, into in ((0, 1, self.a), (1, -1, self.b)):
                self.arrived(part)
                here = self.slot(self.f, part)
                own = self.block(step(self.axis, by), part)
                here[...] = (here[...].astype(F32) + own[...].astype(F32)).astype(BF)
                self.push(here, self.slot(into, part), by)

        def finish(self):
            self.arrived(2, 3, 4, 5)
            total = self.block(at[self.axis], None)[...].astype(F32)
            total = total + self.a[...].astype(F32) + self.b[...].astype(F32)
            self.sent()
            return total

    class DirectScatter(Scatter):
        def start(self):
            for by, into in ((2, self.f), (1, self.a), (-1, self.b)):
                self.push(self.block(step(self.axis, by), None), into, by)

        def finish(self):
            self.arrived(0, 1, 2)
            total = self.block(at[self.axis], None)[...].astype(F32) + self.f[...].astype(F32)
            total = total + self.a[...].astype(F32) + self.b[...].astype(F32)
            self.sent()
            return total

    def grads_out(c):
        for j in range(M // ROWS):
            row = ((j // (N * S) * N + c * S + j % S) * N + j // S % N) * ROWS
            yield pltpu.make_async_copy(full.at[c, pl.ds(j * ROWS, ROWS)], lg_out.at[pl.ds(row, ROWS)], osem.at[c])

    def wait_outs(c):
        pltpu.make_async_copy(full.at[c], lg_out.at[pl.ds(0, M)], osem.at[c]).wait()

        @pl.when(zh // S == c)
        def _():
            pltpu.make_async_copy(sq, sq_out, osem.at[C]).wait()

    def chunk(c):
        def z_send(src):
            for s in range(S):
                @pl.when(zh == c * S + s)
                def _():
                    zbuf[c, s] = src[...]
                    for k in (1, 2, 3):
                        remote(src, zbuf.at[c, s], zsnd.at[k - 1], zrcv.at[c, s], to("zh", k)).start()

        def z_wait(src):
            for s in range(S):
                one = remote(src, zbuf.at[c, s], zsnd.at[0], zrcv.at[c, s], to("zh", 1))

                @pl.when(zh != c * S + s)
                def _():
                    one.wait_recv()

                @pl.when(zh == c * S + s)
                def _():
                    for k in (1, 2, 3):
                        remote(src, zbuf.at[c, s], zsnd.at[k - 1], zrcv.at[c, s], to("zh", k)).wait_send()

            ag[c, y, x] = zbuf[c].astype(F32).reshape(R, depth).astype(BF)

        def gather_stages(src):
            near = [
                DirectGather("x", lambda i, p: ag.at[c, y, i, :, cols(0, p)], agsnd.at[c, 0, 0], agrcv.at[c, 0, 0]),
                DirectGather("y", lambda i, p: ag.at[c, i, x, :, cols(1, p)], agsnd.at[c, 1, 0], agrcv.at[c, 1, 0]),
            ]
            wide = [
                Gather("y", lambda i, p: ag.at[c, i, :, :, cols(0, p)], agsnd.at[c, 0, 1], agrcv.at[c, 0, 1]),
                Gather("x", lambda i, p: ag.at[c, :, i, :, cols(1, p)], agsnd.at[c, 1, 1], agrcv.at[c, 1, 1]),
            ]

            def begin():
                z_wait(src)
                for g in near:
                    g.start()

            def widen():
                for g, w in zip(near, wide):
                    g.finish()
                    w.start()

            def forward():
                for w in wide:
                    w.middle()

            def end():
                for w in wide:
                    w.finish()

            return [begin, widen, forward, end]

        def layer_stages(lhs, rhs, tile):
            copies = {}
            width = feats // PIECES

            def exchange(kind, p, src, dst, peer):
                copies[kind, p] = remote(src, dst, lsnd.at[c, kind, p], lrcv.at[c, kind, p], peer)
                copies[kind, p].start()

            def multiply(p):
                def one(j, carry):
                    where = pl.ds(pl.multiple_of(p * width + j * tile, tile), tile)
                    value = rhs(lhs, where)
                    low, high = value[:HM], value[HM:]
                    keep[c, :, where] = jnp.where(co == 0, low, high)
                    dsend[c, :, where] = jnp.where(co == 0, high, low).astype(BF)
                    return carry

                lax.fori_loop(0, width // tile, one, 0)
                piece = pl.ds(p * width, width)
                exchange(0, p, dsend.at[c, :, piece], drecv.at[c, :, piece], {"co": 1 - co})

            def pair(p):
                copies[0, p].wait()
                piece = pl.ds(p * width, width)
                zs[c, :, piece] = (keep[c, :, piece] + drecv[c, :, piece].astype(F32)).astype(BF)
                exchange(1, p, zs.at[c, :, piece], zv.at[c, :, piece], {"zl": 1 - zl})

            def share(p):
                copies[1, p].wait()
                piece = pl.ds(p * width, width)
                mine = pl.ds(pl.multiple_of(co * HM, HM), HM)
                full[c, mine, piece] = (zs[c, :, piece].astype(F32) + zv[c, :, piece].astype(F32)).astype(BF)
                ref = full.at[c, mine, piece]
                exchange(2, p, ref, ref, {"co": 1 - co})

            def end():
                for p in range(PIECES):
                    copies[2, p].wait()

            pieces = range(PIECES)
            return [
                *[functools.partial(multiply, p) for p in pieces],
                *[functools.partial(pair, p) for p in pieces],
                *[functools.partial(share, p) for p in pieces],
                end,
            ]

        def scatter_stages(multiply):
            wide = [
                Scatter("y", lambda i, p: ps.at[c, i, :, :, cols(0, p)], f1.at[c, 0], a1.at[c, 0], b1.at[c, 0],
                        rssnd.at[c, 0, 0], rsrcv.at[c, 0, 0]),
                Scatter("x", lambda i, p: ps.at[c, :, i, :, cols(1, p)], f1.at[c, 1], a1.at[c, 1], b1.at[c, 1],
                        rssnd.at[c, 1, 0], rsrcv.at[c, 1, 0]),
            ]
            near = [
                DirectScatter(axis, lambda i, p, h=h: ps2.at[c, h, i, :, cols(0, p)], f2.at[c, h], a2.at[c, h], b2.at[c, h],
                        rssnd.at[c, h, 1], rsrcv.at[c, h, 1])
                for h, axis in enumerate(("x", "y"))
            ]

            def begin():
                for h in range(2):
                    multiply(h)
                    wide[h].start()

            def forward():
                for w in wide:
                    w.middle()

            def narrow():
                for h in range(2):
                    ps2[c, h] = wide[h].finish().astype(BF)
                    near[h].start()

            def z_out():
                for h in range(2):
                    ps3[c, :, :, cols(h, None)] = near[h].finish().reshape(S, ROWS, half).astype(BF)
                for s in range(S):
                    @pl.when(zh != c * S + s)
                    def _():
                        k = lax.rem(zh - (c * S + s) + N, N) - 1
                        remote(ps3.at[c, s], zr.at[k], zrsnd.at[c, s], zrrcv.at[k], {"zh": c * S + s}).start()

            return [begin, forward, narrow, z_out]

        def owned(then):
            for s in range(S):
                @pl.when(zh != c * S + s)
                def _():
                    remote(ps3.at[c, s], zr.at[0], zrsnd.at[c, s], zrrcv.at[0], {"zh": c * S + s}).wait_send()

                @pl.when(zh == c * S + s)
                def _():
                    total = ps3[c, s].astype(F32)
                    for k in range(3):
                        remote(ps3.at[c, s], zr.at[k], zrsnd.at[c, s], zrrcv.at[k], to("zh", 1)).wait_recv()
                        total = total + zr[k].astype(F32)
                    then(total)

        def z_first():
            z_send(acts)

        def to_latent():
            preact = full[c].astype(F32) + enc_bias[...]
            gating = jax.nn.sigmoid((preact - threshold[...]) * (1.0 / JUMP))
            value = preact * gating
            lat[c] = value.astype(BF)
            slope[c] = gating + value * (1.0 - gating) * (1.0 / JUMP)

        def to_preact_grad():
            for copy in grads_out(c):
                copy.start()
            lat[c] = (full[c].astype(F32) * slope[c]).astype(BF)

        def to_error():
            def then(total):
                row = lax.broadcasted_iota(jnp.int32, (ROWS, 1), 0)
                first = ((y * N + zh) * N + x) * ROWS
                keeps = jnp.zeros((ROWS, 1), jnp.int32)
                for i in range(ROWS):
                    keeps = jnp.where(row == i, mask[first + i], keeps)
                value = keeps.astype(F32) * (total + dec_bias[...] - acts[...].astype(F32))
                err[...] = value
                errh[...] = value.astype(BF)
                mean = jnp.sum(value * value, axis=1, keepdims=True) * (1.0 / depth)
                lane = lax.broadcasted_iota(jnp.int32, (ROWS, ROWS), 1)
                sq[...] = jnp.sum(jnp.where(row == lane, mean, 0.0), axis=0, keepdims=True)
                pltpu.make_async_copy(sq, sq_out, osem.at[C]).start()

            owned(then)
            z_send(errh)

        def to_input_grad():
            def then(total):
                ig[...] = (total - err[...]).astype(BF)

            wait_outs(c)
            owned(then)

        def dot(a, b, dims):
            return lax.dot_general(a, b, (dims, ((), ())), preferred_element_type=F32)

        def tokens():
            return ag[c].reshape(M, depth)

        def encode(lhs, where):
            return dot(lhs(), enc[:, where], ((1,), (0,)))

        def decode_back(lhs, where):
            return dot(lhs(), dec[where, :], ((1,), (1,)))

        def tiles(h):
            begin = 0
            while begin < half:
                length = min(512, half - begin)
                yield pl.ds(h * half + begin, length), length
                begin += length

        def decode(h):
            for where, length in tiles(h):
                value = dot(lat[c], dec[:, where], ((1,), (0,)))
                ps[c, :, :, :, where] = value.reshape(N, N, R, length).astype(BF)

        def encode_back(h):
            for where, length in tiles(h):
                value = dot(lat[c], enc[where, :], ((1,), (1,)))
                ps[c, :, :, :, where] = value.reshape(N, N, R, length).astype(BF)

        def wait_enc():
            if c == 0:
                enc_copy.wait()

        def wait_dec():
            if c == 0:
                for copy in (dec_copy, *small):
                    copy.wait()

        def joined(*parts):
            def run():
                for part in parts:
                    part()

            return run

        g1, l1, s1 = gather_stages(acts), layer_stages(tokens, encode, 256), scatter_stages(decode)
        g2, l2, s2 = gather_stages(errh), layer_stages(tokens, decode_back, 256), scatter_stages(encode_back)
        return [
            z_first,
            *g1[:-1],
            joined(g1[-1], wait_enc, l1[0]),
            *l1[1:-1],
            joined(l1[-1], wait_dec, to_latent, s1[0]),
            *s1[1:],
            to_error,
            *g2[:-1],
            joined(g2[-1], l2[0]),
            *l2[1:-1],
            joined(l2[-1], to_preact_grad, s2[0]),
            *s2[1:],
            to_input_grad,
        ]

    plans = [iter(chunk(c)) for c in range(C)]
    for c in TURNS:
        next(plans[c])()
    assert all(next(plan, None) is None for plan in plans)
    ig_copy = pltpu.make_async_copy(ig, ig_out, osem.at[C])
    ig_copy.start()
    ig_copy.wait()


def finish(sq_hbm, ig_hbm, lg_hbm, sq_out, ig_out, lg_out, sq, ig, raw, wide, isem, osem):
    parts = isem.shape[0] - 2
    length = raw.shape[0] // parts

    def rows(p):
        return pl.ds(p * length, length)

    ins = [pltpu.make_async_copy(lg_hbm.at[rows(p)], raw.at[rows(p)], isem.at[p]) for p in range(parts)]
    ins += [pltpu.make_async_copy(src, dst, isem.at[parts + n]) for n, (src, dst) in enumerate(((sq_hbm, sq), (ig_hbm, ig)))]
    outs = [pltpu.make_async_copy(wide.at[rows(p)], lg_out.at[rows(p)], osem.at[p]) for p in range(parts)]
    outs += [pltpu.make_async_copy(src, dst, osem.at[parts + n]) for n, (src, dst) in enumerate(((sq, sq_out), (ig, ig_out)))]
    for copy in ins:
        copy.start()
    for p in range(parts):
        ins[p].wait()
        wide[rows(p)] = raw[rows(p)].astype(F32)
        outs[p].start()
    for n in (parts, parts + 1):
        ins[n].wait()
        outs[n].start()
    for copy in outs:
        copy.wait()


def shards(activations, enc_weight, dec_weight, enc_bias, threshold, dec_bias, token_mask):
    depth, feats = enc_weight.shape[1:]
    half = depth // 2
    hbm = pl.BlockSpec(memory_space=pltpu.HBM)
    dma = pltpu.SemaphoreType.DMA
    scratch = [
        pltpu.VMEM((ROWS, depth), BF),
        *[pltpu.VMEM((1, feats), F32)] * 2,
        pltpu.VMEM((1, depth), F32),
        pltpu.SMEM(token_mask.shape, jnp.int32),
        pltpu.VMEM((depth, feats), BF),
        pltpu.VMEM((feats, depth), BF),
        pltpu.VMEM((C, N, N, R, depth), BF),
        pltpu.VMEM((C, S, ROWS, depth), BF),
        pltpu.VMEM((C, N, N, R, depth), BF),
        *[pltpu.VMEM((C, 2, N, R, half), BF)] * 3,
        pltpu.VMEM((C, 2, N, R, half), BF),
        *[pltpu.VMEM((C, 2, R, half), BF)] * 3,
        pltpu.VMEM((C, S, ROWS, depth), BF),
        pltpu.VMEM((N - 1, ROWS, depth), BF),
        pltpu.VMEM((C, HM, feats), F32),
        *[pltpu.VMEM((C, HM, feats), BF)] * 4,
        pltpu.VMEM((C, M, feats), BF),
        pltpu.VMEM((C, M, feats), BF),
        pltpu.VMEM((C, M, feats), F32),
        pltpu.VMEM((ROWS, depth), F32),
        pltpu.VMEM((ROWS, depth), BF),
        pltpu.VMEM((1, ROWS), F32),
        pltpu.VMEM((ROWS, depth), BF),
        dma((7,)),
        dma((C + 1,)),
        dma((3,)), dma((C, S)),
        dma((C, 2, 2, 6)), dma((C, 2, 2, 6)),
        dma((C, 2, 2, 6)), dma((C, 2, 2, 6)),
        dma((C, S)), dma((3,)),
        dma((C, 3, PIECES)), dma((C, 3, PIECES)),
    ]
    sq, ig, lg = pl.pallas_call(
        kernel,
        out_shape=(
            jax.ShapeDtypeStruct((1, ROWS), F32),
            jax.ShapeDtypeStruct((ROWS, depth), BF),
            jax.ShapeDtypeStruct((N * N * N * ROWS, feats), BF),
        ),
        in_specs=[hbm] * 7,
        out_specs=(hbm,) * 3,
        scratch_shapes=scratch,
        compiler_params=pltpu.CompilerParams(
            collective_id=0, has_side_effects=True, vmem_limit_bytes=67043328
        ),
    )(
        activations[:, 0], enc_weight[0], dec_weight[0], enc_bias[None], threshold[None], dec_bias, token_mask,
    )
    tokens, parts = N * N * N * ROWS, 4
    sq, ig, lg = pl.pallas_call(
        finish,
        out_shape=(
            jax.ShapeDtypeStruct((1, ROWS), F32),
            jax.ShapeDtypeStruct((ROWS, depth), BF),
            jax.ShapeDtypeStruct((tokens, feats), F32),
        ),
        in_specs=[hbm] * 3,
        out_specs=(hbm,) * 3,
        scratch_shapes=[
            pltpu.VMEM((1, ROWS), F32),
            pltpu.VMEM((ROWS, depth), BF),
            pltpu.VMEM((tokens, feats), BF),
            pltpu.VMEM((tokens, feats), F32),
            dma((parts + 2,)), dma((parts + 2,)),
        ],
        compiler_params=pltpu.CompilerParams(vmem_limit_bytes=67043328),
    )(sq, ig, lg)
    return sq.reshape(ROWS, 1), lg, ig[:, None]


def solution(mesh):
    finer = Mesh(mesh.devices.reshape(2, 2, N, N, N), LAYER + FEAT)
    return jax.shard_map(
        shards,
        mesh=finer,
        in_specs=(
            P(FEAT, LAYER, None),
            P(LAYER, None, FEAT),
            P(LAYER, FEAT, None),
            P(FEAT),
            P(FEAT),
            P(LAYER, None),
            P(),
        ),
        out_specs=(P(FEAT, LAYER), P(None, FEAT), P(FEAT, LAYER, None)),
        check_vma=False,
    )
```

time: 147 us -> 115 us (0.78)
  Pallas kernels: 136 us -> 114 us
  local copies, waits for them, and re-layouts: 8.51 us -> 0 us
    pallas_call x1 -> x2, Pallas kernels: 136 us -> 114 us  [the longest x1 112 us: shards(): pl.pallas_call(kernel, out_shape=(jax.ShapeDtypeStruct((1, ROWS), F32), j...]
    unnamed x14 -> x0, local copies, waits for them, and re-layouts: 7.05 us -> none
where the time goes in v2:
time: 115 us
  Pallas kernels  114 us (99%)
    pallas_call x1, Pallas kernels, shards(): pl.pallas_call(kernel, out_shape=(jax.ShapeDtypeStruct((1, ROWS), F32), j...  112 us
    pallas_call x1, Pallas kernels, shards(): pl.pallas_call(finish, out_shape=(jax.ShapeDtypeStruct((1, ROWS), F32), j...  2.4 us

profile of v2, /device:TPU:64, one launch (start us, length us, event | category | flops | bytes accessed | tf_op | source)
XLA Modules:
  0.0 114.7 jit_solution(15578968691105440171)
XLA Ops:
  0.6 111.5 %shard_map.94 = (f32[1,8]{1,0:T(1,128)}, bf16[8,2304]{1,0:T(8,128)(2,1)}, bf16[512,1024]{1,0:T(8,128)(2,1)}) custom-call(bf16[8,2304]{1,0:T(8,128)(2,1)} %bitcast.9, bf16[2304,1024]{1,0:T(8,128)(2,1)} %bitcast.7, bf16[1024,2304]{1,0:T(8,128)(2,1)} %bitcast.8, f32[1,1024]{1,0:T(1,128)} %bitcast.10, f32[1,1024]{1,0:T(1,128)} %bitcast.11, ...), custom_call_target="tpu_custom_call" | custom-call | tf_op jit(solution)/shard_map/pallas_call | solution.py:514
  112.2 2.4 %shard_map.95 = (f32[1,8]{1,0:T(1,128)}, bf16[8,2304]{1,0:T(8,128)(2,1)}, f32[512,1024]{1,0:T(8,128)}) custom-call(f32[1,8]{1,0:T(1,128)} %get-tuple-element.9.sq_hbm, bf16[8,2304]{1,0:T(8,128)(2,1)} %get-tuple-element.10.ig_hbm, bf16[512,1024]{1,0:T(8,128)(2,1)} %get-tuple-element.11.lg_hbm), custom_call_target="tpu_custom_call" | custom-call | tf_op jit(solution)/shard_map/pallas_call | solution.py:531

commit v3 on v2

--- a/solution.py
+++ b/solution.py
@@ -24,19 +24,19 @@
 HM = M // 2
 PIECES = 2
 TURNS = (
-    0, 2, 1, 3, 0, 2, 1, 3, 0, 1, 0, 2, 1, 3, 0, 2, 0, 0, 1, 0, 3, 1, 1, 1, 2, 0, 2, 0, 2,
-    3, 2, 0, 3, 1, 1, 3, 1, 0, 2, 3, 2, 2, 3, 1, 0, 2, 1, 3, 0, 2, 3, 1, 2, 0, 3, 1, 3, 2,
-    0, 1, 3, 0, 2, 1, 0, 3, 1, 2, 0, 3, 0, 0, 2, 1, 0, 1, 3, 1, 2, 0, 1, 2, 3, 2, 0, 2, 1,
-    0, 1, 3, 3, 3, 2, 2, 0, 3, 1, 2, 3, 3, 0, 3, 2, 0, 1, 3, 2, 1, 3, 2, 1, 3, 2, 1, 0, 3,
+    0, 2, 3, 1, 0, 2, 4, 3, 0, 2, 4, 0, 1, 2, 3, 0, 0, 1, 0, 2, 2, 3, 0, 2, 0, 2, 3, 1, 0, 3,
+    3, 0, 3, 2, 2, 1, 1, 2, 1, 1, 3, 3, 0, 2, 3, 0, 1, 1, 2, 1, 3, 0, 1, 2, 3, 0, 1, 2, 3, 1,
+    0, 2, 3, 0, 1, 2, 3, 0, 1, 2, 3, 0, 0, 1, 0, 0, 2, 3, 2, 2, 1, 0, 2, 3, 3, 3, 0, 1, 1, 3,
+    2, 0, 2, 1, 1, 2, 3, 3, 0, 3, 1, 1, 2, 1, 3, 1, 0, 2, 3, 1, 2, 0, 3, 1, 3, 0, 2, 1,
 )
 
 
 def kernel(
     acts_hbm, enc_hbm, dec_hbm, enc_bias_hbm, threshold_hbm, dec_bias_hbm, mask_hbm,
     sq_out, ig_out, lg_out,
-    acts, enc_bias, threshold, dec_bias, mask, enc, dec, ag, zbuf, ps, f1, a1, b1, ps2, f2, a2, b2, ps3, zr,
+    acts, enc_bias, threshold, dec_bias, mask, enc, dec, enc_t, dec_t, ag, zbuf, ps, r1, ps2, r2, ps3, zr,
     keep, dsend, drecv, zs, zv, full, lat, slope, err, errh, sq, ig,
-    wsem, osem, zsnd, zrcv, agsnd, agrcv, rssnd, rsrcv, zrsnd, zrrcv, lsnd, lrcv,
+    wsem, osem, zsnd, zrcv, snd, gn, gw, sw, sn, zrsnd, zrrcv, lsnd, lrcv,
 ):
     depth = ag.shape[-1]
     feats = lat.shape[-1]
@@ -81,23 +81,29 @@
         return pl.ds(h * half + base, length)
 
     class Ring:
-        def __init__(self, axis, block, send, recv):
-            self.axis, self.block, self.send, self.recv = axis, block, send, recv
+        def __init__(self, axis, block, size, send, recv):
+            self.axis, self.block, self.size, self.send, self.recv = axis, block, size, send, recv
             self.copies = []
 
         def push(self, src, dst, by):
-            n = len(self.copies)
-            copy = remote(src, dst, self.send.at[n], self.recv.at[n], to(self.axis, by))
+            recv = self.recv.at[min(len(self.copies), self.recv.shape[0] - 1)]
+            copy = remote(src, dst, self.send, recv, to(self.axis, by))
             copy.start()
             self.copies.append(copy)
 
-        def arrived(self, *which):
-            for n in which:
-                self.copies[n].wait_recv()
+        def wait(self, blocks, sem):
+            ref = self.size.at[pl.ds(0, blocks)]
+            pltpu.make_async_copy(ref, ref, sem).wait()
+
+        def first(self, n):
+            self.copies[n].wait_recv()
+
+        def rest(self):
+            last = self.recv.shape[0] - 1
+            self.wait(3 if last == 0 else 2, self.recv.at[last])
 
         def sent(self):
-            for copy in self.copies:
-                copy.wait_send()
+            self.wait(3, self.send)
 
     class Gather(Ring):
         def pass_on(self, pos, part, by):
@@ -112,13 +118,13 @@
             self.pass_on(me, 0, -1)
 
         def middle(self):
-            self.arrived(0)
+            self.first(0)
             self.pass_on(step(self.axis, -1), 0, 1)
-            self.arrived(1)
+            self.first(1)
             self.pass_on(step(self.axis, 1), 1, -1)
 
         def finish(self):
-            self.arrived(2, 3, 4, 5)
+            self.rest()
             self.sent()
 
     class DirectGather(Ring):
@@ -128,13 +134,13 @@
                 self.push(ref, ref, by)
 
         def finish(self):
-            self.arrived(0, 1, 2)
+            self.rest()
             self.sent()
 
     class Scatter(Ring):
-        def __init__(self, axis, block, f, a, b, send, recv):
-            super().__init__(axis, block, send, recv)
-            self.f, self.a, self.b = f, a, b
+        def __init__(self, axis, block, size, send, recv):
+            super().__init__(axis, block, size, send, recv)
+            self.f, self.a, self.b = (size.at[n] for n in range(3))
 
         def slot(self, buf, part):
             return buf.at[(slice(None),) * (len(buf.shape) - 1) + (cols(0, part),)]
@@ -148,14 +154,14 @@
 
         def middle(self):
             for part, by, into in ((0, 1, self.a), (1, -1, self.b)):
-                self.arrived(part)
+                self.first(part)
                 here = self.slot(self.f, part)
                 own = self.block(step(self.axis, by), part)
                 here[...] = (here[...].astype(F32) + own[...].astype(F32)).astype(BF)
                 self.push(here, self.slot(into, part), by)
 
         def finish(self):
-            self.arrived(2, 3, 4, 5)
+            self.rest()
             total = self.block(at[self.axis], None)[...].astype(F32)
             total = total + self.a[...].astype(F32) + self.b[...].astype(F32)
             self.sent()
@@ -167,7 +173,7 @@
                 self.push(self.block(step(self.axis, by), None), into, by)
 
         def finish(self):
-            self.arrived(0, 1, 2)
+            self.rest()
             total = self.block(at[self.axis], None)[...].astype(F32) + self.f[...].astype(F32)
             total = total + self.a[...].astype(F32) + self.b[...].astype(F32)
             self.sent()
@@ -211,12 +217,12 @@
 
         def gather_stages(src):
             near = [
-                DirectGather("x", lambda i, p: ag.at[c, y, i, :, cols(0, p)], agsnd.at[c, 0, 0], agrcv.at[c, 0, 0]),
-                DirectGather("y", lambda i, p: ag.at[c, i, x, :, cols(1, p)], agsnd.at[c, 1, 0], agrcv.at[c, 1, 0]),
+                DirectGather("x", lambda i, p: ag.at[c, y, i, :, cols(0, p)], r2.at[c, 0], snd.at[c, 0], gn.at[c, 0]),
+                DirectGather("y", lambda i, p: ag.at[c, i, x, :, cols(1, p)], r2.at[c, 1], snd.at[c, 1], gn.at[c, 1]),
             ]
             wide = [
-                Gather("y", lambda i, p: ag.at[c, i, :, :, cols(0, p)], agsnd.at[c, 0, 1], agrcv.at[c, 0, 1]),
-                Gather("x", lambda i, p: ag.at[c, :, i, :, cols(1, p)], agsnd.at[c, 1, 1], agrcv.at[c, 1, 1]),
+                Gather("y", lambda i, p: ag.at[c, i, :, :, cols(0, p)], r1.at[c, 0], snd.at[c, 0], gw.at[c, 0]),
+                Gather("x", lambda i, p: ag.at[c, :, i, :, cols(1, p)], r1.at[c, 1], snd.at[c, 1], gw.at[c, 1]),
             ]
 
             def begin():
@@ -239,25 +245,20 @@
 
             return [begin, widen, forward, end]
 
-        def layer_stages(lhs, rhs, tile):
+        def layer_stages(lhs, product):
             copies = {}
             width = feats // PIECES
 
             def exchange(kind, p, src, dst, peer):
-                copies[kind, p] = remote(src, dst, lsnd.at[c, kind, p], lrcv.at[c, kind, p], peer)
+                copies[kind, p] = remote(src, dst, lsnd.at[c, p], lrcv.at[c, kind, p], peer)
                 copies[kind, p].start()
 
             def multiply(p):
-                def one(j, carry):
-                    where = pl.ds(pl.multiple_of(p * width + j * tile, tile), tile)
-                    value = rhs(lhs, where)
-                    low, high = value[:HM], value[HM:]
-                    keep[c, :, where] = jnp.where(co == 0, low, high)
-                    dsend[c, :, where] = jnp.where(co == 0, high, low).astype(BF)
-                    return carry
-
-                lax.fori_loop(0, width // tile, one, 0)
                 piece = pl.ds(p * width, width)
+                value = product(lhs, piece)
+                low, high = value[:HM], value[HM:]
+                keep[c, :, piece] = jnp.where(co == 0, low, high)
+                dsend[c, :, piece] = jnp.where(co == 0, high, low).astype(BF)
                 exchange(0, p, dsend.at[c, :, piece], drecv.at[c, :, piece], {"co": 1 - co})
 
             def pair(p):
@@ -288,14 +289,11 @@
 
         def scatter_stages(multiply):
             wide = [
-                Scatter("y", lambda i, p: ps.at[c, i, :, :, cols(0, p)], f1.at[c, 0], a1.at[c, 0], b1.at[c, 0],
-                        rssnd.at[c, 0, 0], rsrcv.at[c, 0, 0]),
-                Scatter("x", lambda i, p: ps.at[c, :, i, :, cols(1, p)], f1.at[c, 1], a1.at[c, 1], b1.at[c, 1],
-                        rssnd.at[c, 1, 0], rsrcv.at[c, 1, 0]),
+                Scatter("y", lambda i, p: ps.at[c, i, :, :, cols(0, p)], r1.at[c, 0], snd.at[c, 0], sw.at[c, 0]),
+                Scatter("x", lambda i, p: ps.at[c, :, i, :, cols(1, p)], r1.at[c, 1], snd.at[c, 1], sw.at[c, 1]),
             ]
             near = [
-                DirectScatter(axis, lambda i, p, h=h: ps2.at[c, h, i, :, cols(0, p)], f2.at[c, h], a2.at[c, h], b2.at[c, h],
-                        rssnd.at[c, h, 1], rsrcv.at[c, h, 1])
+                DirectScatter(axis, lambda i, p, h=h: ps2.at[c, h, i, :, cols(0, p)], r2.at[c, h], snd.at[c, h], sn.at[c, h])
                 for h, axis in enumerate(("x", "y"))
             ]
 
@@ -378,17 +376,17 @@
             wait_outs(c)
             owned(then)
 
-        def dot(a, b, dims):
-            return lax.dot_general(a, b, (dims, ((), ())), preferred_element_type=F32)
+        def dot(a, b):
+            return jnp.dot(a, b, preferred_element_type=F32)
 
         def tokens():
             return ag[c].reshape(M, depth)
 
         def encode(lhs, where):
-            return dot(lhs(), enc[:, where], ((1,), (0,)))
+            return dot(lhs(), enc[:, where])
 
         def decode_back(lhs, where):
-            return dot(lhs(), dec[where, :], ((1,), (1,)))
+            return dot(lhs(), dec_t[:, where])
 
         def tiles(h):
             begin = 0
@@ -399,22 +397,13 @@
 
         def decode(h):
             for where, length in tiles(h):
-                value = dot(lat[c], dec[:, where], ((1,), (0,)))
+                value = dot(lat[c], dec[:, where])
                 ps[c, :, :, :, where] = value.reshape(N, N, R, length).astype(BF)
 
         def encode_back(h):
             for where, length in tiles(h):
-                value = dot(lat[c], enc[where, :], ((1,), (1,)))
+                value = dot(lat[c], enc_t[:, where])
                 ps[c, :, :, :, where] = value.reshape(N, N, R, length).astype(BF)
-
-        def wait_enc():
-            if c == 0:
-                enc_copy.wait()
-
-        def wait_dec():
-            if c == 0:
-                for copy in (dec_copy, *small):
-                    copy.wait()
 
         def joined(*parts):
             def run():
@@ -423,14 +412,14 @@
 
             return run
 
-        g1, l1, s1 = gather_stages(acts), layer_stages(tokens, encode, 256), scatter_stages(decode)
-        g2, l2, s2 = gather_stages(errh), layer_stages(tokens, decode_back, 256), scatter_stages(encode_back)
+        g1, l1, s1 = gather_stages(acts), layer_stages(tokens, encode), scatter_stages(decode)
+        g2, l2, s2 = gather_stages(errh), layer_stages(tokens, decode_back), scatter_stages(encode_back)
         return [
             z_first,
             *g1[:-1],
-            joined(g1[-1], wait_enc, l1[0]),
+            joined(g1[-1], l1[0]),
             *l1[1:-1],
-            joined(l1[-1], wait_dec, to_latent, s1[0]),
+            joined(l1[-1], to_latent, s1[0]),
             *s1[1:],
             to_error,
             *g2[:-1],
@@ -441,7 +430,22 @@
             to_input_grad,
         ]
 
-    plans = [iter(chunk(c)) for c in range(C)]
+    def turned(copies, src, dst):
+        for copy in copies:
+            copy.wait()
+
+        def one(j, carry):
+            where = pl.ds(pl.multiple_of(j * 256, 256), 256)
+            dst[:, where] = src[where, :].T
+            return carry
+
+        lax.fori_loop(0, src.shape[0] // 256, one, 0)
+
+    weights = [
+        functools.partial(turned, [enc_copy], enc, enc_t),
+        functools.partial(turned, [dec_copy, *small], dec, dec_t),
+    ]
+    plans = [iter(chunk(c)) for c in range(C)] + [iter(weights)]
     for c in TURNS:
         next(plans[c])()
     assert all(next(plan, None) is None for plan in plans)
@@ -486,12 +490,14 @@
         pltpu.SMEM(token_mask.shape, jnp.int32),
         pltpu.VMEM((depth, feats), BF),
         pltpu.VMEM((feats, depth), BF),
+        pltpu.VMEM((feats, depth), BF),
+        pltpu.VMEM((depth, feats), BF),
         pltpu.VMEM((C, N, N, R, depth), BF),
         pltpu.VMEM((C, S, ROWS, depth), BF),
         pltpu.VMEM((C, N, N, R, depth), BF),
-        *[pltpu.VMEM((C, 2, N, R, half), BF)] * 3,
+        pltpu.VMEM((C, 2, 3, N, R, half), BF),
         pltpu.VMEM((C, 2, N, R, half), BF),
-        *[pltpu.VMEM((C, 2, R, half), BF)] * 3,
+        pltpu.VMEM((C, 2, 3, R, half), BF),
         pltpu.VMEM((C, S, ROWS, depth), BF),
         pltpu.VMEM((N - 1, ROWS, depth), BF),
         pltpu.VMEM((C, HM, feats), F32),
@@ -506,10 +512,10 @@
         dma((7,)),
         dma((C + 1,)),
         dma((3,)), dma((C, S)),
-        dma((C, 2, 2, 6)), dma((C, 2, 2, 6)),
-        dma((C, 2, 2, 6)), dma((C, 2, 2, 6)),
+        dma((C, 2)),
+        dma((C, 2, 1)), dma((C, 2, 3)), dma((C, 2, 3)), dma((C, 2, 1)),
         dma((C, S)), dma((3,)),
-        dma((C, 3, PIECES)), dma((C, 3, PIECES)),
+        dma((C, PIECES)), dma((C, 3, PIECES)),
     ]
     sq, ig, lg = pl.pallas_call(
         kernel,

time: 115 us -> 108 us (0.939)
  Pallas kernels: 114 us -> 108 us
    pallas_call x1, Pallas kernels: 112 us -> 105 us  [shards(): pl.pallas_call(kernel, out_shape=(jax.ShapeDtypeStruct((1, ROWS), F32), j...]
where the time goes in v3:
time: 108 us
  Pallas kernels  108 us (100%)
    pallas_call x1, Pallas kernels, shards(): pl.pallas_call(kernel, out_shape=(jax.ShapeDtypeStruct((1, ROWS), F32), j...  105 us
    pallas_call x1, Pallas kernels, shards(): pl.pallas_call(finish, out_shape=(jax.ShapeDtypeStruct((1, ROWS), F32), j...  2.4 us

profile of v3, /device:TPU:64, one launch (start us, length us, event | category | flops | bytes accessed | tf_op | source)
XLA Modules:
  0.0 108.4 jit_solution(10782284953044653749)
XLA Ops:
  0.6 105.2 %shard_map.94 = (f32[1,8]{1,0:T(1,128)}, bf16[8,2304]{1,0:T(8,128)(2,1)}, bf16[512,1024]{1,0:T(8,128)(2,1)}) custom-call(bf16[8,2304]{1,0:T(8,128)(2,1)} %bitcast.9, bf16[2304,1024]{1,0:T(8,128)(2,1)} %bitcast.7, bf16[1024,2304]{1,0:T(8,128)(2,1)} %bitcast.8, f32[1,1024]{1,0:T(1,128)} %bitcast.10, f32[1,1024]{1,0:T(1,128)} %bitcast.11, ...), custom_call_target="tpu_custom_call" | custom-call | tf_op jit(solution)/shard_map/pallas_call | solution.py:520
  105.8 2.4 %shard_map.95 = (f32[1,8]{1,0:T(1,128)}, bf16[8,2304]{1,0:T(8,128)(2,1)}, f32[512,1024]{1,0:T(8,128)}) custom-call(f32[1,8]{1,0:T(1,128)} %get-tuple-element.9.sq_hbm, bf16[8,2304]{1,0:T(8,128)(2,1)} %get-tuple-element.10.ig_hbm, bf16[512,1024]{1,0:T(8,128)(2,1)} %get-tuple-element.11.lg_hbm), custom_call_target="tpu_custom_call" | custom-call | tf_op jit(solution)/shard_map/pallas_call | solution.py:537

commit v4 on v3

--- a/solution.py
+++ b/solution.py
@@ -245,12 +245,12 @@
 
             return [begin, widen, forward, end]
 
-        def layer_stages(lhs, product):
+        def layer_stages(turn, lhs, product):
             copies = {}
             width = feats // PIECES
 
             def exchange(kind, p, src, dst, peer):
-                copies[kind, p] = remote(src, dst, lsnd.at[c, p], lrcv.at[c, kind, p], peer)
+                copies[kind, p] = remote(src, dst, lsnd.at[c, p], lrcv.at[c, 3 if kind == 1 and turn else kind, p], peer)
                 copies[kind, p].start()
 
             def multiply(p):
@@ -265,13 +265,13 @@
                 copies[0, p].wait()
                 piece = pl.ds(p * width, width)
                 zs[c, :, piece] = (keep[c, :, piece] + drecv[c, :, piece].astype(F32)).astype(BF)
-                exchange(1, p, zs.at[c, :, piece], zv.at[c, :, piece], {"zl": 1 - zl})
+                exchange(1, p, zs.at[c, :, piece], zv.at[turn, c, :, piece], {"zl": 1 - zl})
 
             def share(p):
                 copies[1, p].wait()
                 piece = pl.ds(p * width, width)
                 mine = pl.ds(pl.multiple_of(co * HM, HM), HM)
-                full[c, mine, piece] = (zs[c, :, piece].astype(F32) + zv[c, :, piece].astype(F32)).astype(BF)
+                full[c, mine, piece] = (zs[c, :, piece].astype(F32) + zv[turn, c, :, piece].astype(F32)).astype(BF)
                 ref = full.at[c, mine, piece]
                 exchange(2, p, ref, ref, {"co": 1 - co})
 
@@ -412,8 +412,8 @@
 
             return run
 
-        g1, l1, s1 = gather_stages(acts), layer_stages(tokens, encode), scatter_stages(decode)
-        g2, l2, s2 = gather_stages(errh), layer_stages(tokens, decode_back), scatter_stages(encode_back)
+        g1, l1, s1 = gather_stages(acts), layer_stages(0, tokens, encode), scatter_stages(decode)
+        g2, l2, s2 = gather_stages(errh), layer_stages(1, tokens, decode_back), scatter_stages(encode_back)
         return [
             z_first,
             *g1[:-1],
@@ -501,7 +501,8 @@
         pltpu.VMEM((C, S, ROWS, depth), BF),
         pltpu.VMEM((N - 1, ROWS, depth), BF),
         pltpu.VMEM((C, HM, feats), F32),
-        *[pltpu.VMEM((C, HM, feats), BF)] * 4,
+        *[pltpu.VMEM((C, HM, feats), BF)] * 3,
+        pltpu.VMEM((2, C, HM, feats), BF),
         pltpu.VMEM((C, M, feats), BF),
         pltpu.VMEM((C, M, feats), BF),
         pltpu.VMEM((C, M, feats), F32),
@@ -515,7 +516,7 @@
         dma((C, 2)),
         dma((C, 2, 1)), dma((C, 2, 3)), dma((C, 2, 3)), dma((C, 2, 1)),
         dma((C, S)), dma((3,)),
-        dma((C, PIECES)), dma((C, 3, PIECES)),
+        dma((C, PIECES)), dma((C, 4, PIECES)),
     ]
     sq, ig, lg = pl.pallas_call(
         kernel,

time: 108 us -> 109 us (level)
  no operation moved by 1% of the time
where the time goes in v4:
time: 109 us; the launch traced here: 108 us
  Pallas kernels  108 us (99%)
    pallas_call x1, Pallas kernels, shards(): pl.pallas_call(kernel, out_shape=(jax.ShapeDtypeStruct((1, ROWS), F32), j...  105 us
    pallas_call x1, Pallas kernels, shards(): pl.pallas_call(finish, out_shape=(jax.ShapeDtypeStruct((1, ROWS), F32), j...  2.4 us

profile of v4, /device:TPU:64, one launch (start us, length us, event | category | flops | bytes accessed | tf_op | source)
XLA Modules:
  0.0 108.5 jit_solution(16225619164701269032)
XLA Ops:
  0.6 105.3 %shard_map.94 = (f32[1,8]{1,0:T(1,128)}, bf16[8,2304]{1,0:T(8,128)(2,1)}, bf16[512,1024]{1,0:T(8,128)(2,1)}) custom-call(bf16[8,2304]{1,0:T(8,128)(2,1)} %bitcast.9, bf16[2304,1024]{1,0:T(8,128)(2,1)} %bitcast.7, bf16[1024,2304]{1,0:T(8,128)(2,1)} %bitcast.8, f32[1,1024]{1,0:T(1,128)} %bitcast.10, f32[1,1024]{1,0:T(1,128)} %bitcast.11, ...), custom_call_target="tpu_custom_call" | custom-call | tf_op jit(solution)/shard_map/pallas_call | solution.py:521
  105.9 2.4 %shard_map.95 = (f32[1,8]{1,0:T(1,128)}, bf16[8,2304]{1,0:T(8,128)(2,1)}, f32[512,1024]{1,0:T(8,128)}) custom-call(f32[1,8]{1,0:T(1,128)} %get-tuple-element.9.sq_hbm, bf16[8,2304]{1,0:T(8,128)(2,1)} %get-tuple-element.10.ig_hbm, bf16[512,1024]{1,0:T(8,128)(2,1)} %get-tuple-element.11.lg_hbm), custom_call_target="tpu_custom_call" | custom-call | tf_op jit(solution)/shard_map/pallas_call | solution.py:538
